TPU v7x, 32 devices: a whole 2x2x4 slice. The times are simulated.
32 devices in a mesh: row: 8 (over y, x, core), col: 4 (over z).
Axes of the slice: x: 2, y: 2, z: 4, core: 2. Of those that a mesh axis runs over, the one named last changes fastest.
Arguments:
- density_start: float32 [512, 512], P('row', 'col'), may hold values from -0.5 to 1, as said below
- branches: int32 [6], replicated, may hold values from 0 to 1, as said below
Outputs:
- density: float32 [512, 512], P('row', 'col')
- occupations: float32 [6, 2], replicated
Inputs may be any that keep to these rules, and one draw needn't show every extreme that they name: density_start is symmetric with eigenvalues inside 0 to 1. `branches`: each entry is 0 or 1, and exactly 3 entries are 1.
All inputs are finite; a program needn't handle non-finite values.
Results may differ from a plain program's by a relative error of at most 0.0025.
Values may be sent and summed in bfloat16 or wider, within the bound.
A program may use at most 64 MiB of HBM per device.

v0:
```python
import jax
import jax.numpy as jnp
from jax import lax
from jax.sharding import PartitionSpec as P

ITERS = 6


def taken_in(shard, axis, dim, absorb, state):
    everything = jax.tree.map(lambda a: lax.all_gather(a, axis, axis=dim, tiled=True), shard)
    return absorb(state, everything, jnp.int32(0))


def local_trace(matrix_block, diagonal_mask):
    return jnp.sum(matrix_block * diagonal_mask)


def body(density_start, branches):
    rows_here, cols_here = density_start.shape
    row_first = lax.axis_index("row") * rows_here
    col_first = lax.axis_index("col") * cols_here
    row_ids = row_first + lax.broadcasted_iota(jnp.int32, (rows_here, cols_here), 0)
    col_ids = col_first + lax.broadcasted_iota(jnp.int32, (rows_here, cols_here), 1)
    diagonal_mask = (row_ids == col_ids).astype(jnp.float32)
    size_total = cols_here * lax.axis_size("col")
    density = density_start
    records = []
    for iteration in range(ITERS):
        narrow = density.astype(jnp.bfloat16)
        empty = jnp.zeros((rows_here, cols_here), jnp.float32)
        plain_local = local_trace(density, diagonal_mask)
        row_panel = lax.all_gather(narrow, "col", axis=1, tiled=True)

        def add_rows(accumulated, shard_piece, offset):
            panel_part = lax.dynamic_slice_in_dim(row_panel, offset, shard_piece.shape[0], 1)
            return accumulated + jnp.dot(
                panel_part, shard_piece, preferred_element_type=jnp.float32
            )

        square = taken_in(narrow, "row", 0, add_rows, empty)
        square_local = local_trace(square, diagonal_mask)
        branch_now = branches[iteration]
        records.append(jnp.stack([plain_local, square_local]))
        density = jnp.where(branch_now == 1, 2.0 * density - square, square)
    stacked = jnp.stack(records)
    stacked = lax.psum(stacked, ("row", "col"))
    occupations = stacked / size_total
    return (density, occupations)


def solution(mesh):
    in_specs = (P("row", "col"), P())
    out_specs = (P("row", "col"), P())
    return jax.shard_map(body, mesh=mesh, in_specs=in_specs, out_specs=out_specs, check_vma=False)
```

profile of v0, /device:TPU:0, one launch (start us, length us, event | category | flops | bytes accessed | tf_op | source)
XLA Modules:
  0.0 182.0 jit_solution(16147823306401190443)
XLA Ops:
  0.6 0.0 copy-start
  0.7 1.6 fusion.17
  6.1 0.0 copy-done
  6.1 13.7 %all_gather.36 = bf16[64,512]{1,0:T(8,128)(2,1)S(1)} all-gather(bf16[64,128]{1,0:T(8,128)(2,1)S(1)} %convert_element_type.19), channel_id=1, replica_groups=mesh['row'=8,'col'=4] {'col'}, dimensions={1}, use_global_device_ids=true | all-gather | bytes 81920 | tf_op jit(solution)/shard_map/all_gather | solution.py:32
  19.8 9.2 %all_gather.37 = bf16[512,128]{1,0:T(8,128)(2,1)S(1)} all-gather(bf16[64,128]{1,0:T(8,128)(2,1)S(1)} %convert_element_type.19), channel_id=1, replica_groups=mesh['row'=8,'col'=4] {'row'}, dimensions={0}, use_global_device_ids=true | all-gather | bytes 147456 | tf_op jit(solution)/shard_map/all_gather | solution.py:10
  29.0 0.2 fusion.16
  29.2 12.0 %all_gather.38 = bf16[64,512]{1,0:T(8,128)(2,1)S(1)} all-gather(bf16[64,128]{1,0:T(8,128)(2,1)S(1)} %get-tuple-element.24), channel_id=1, replica_groups=mesh['row'=8,'col'=4] {'col'}, dimensions={1}, use_global_device_ids=true | all-gather | bytes 81920 | tf_op jit(solution)/shard_map/all_gather | solution.py:32
  41.2 9.2 %all_gather.39 = bf16[512,128]{1,0:T(8,128)(2,1)S(1)} all-gather(bf16[64,128]{1,0:T(8,128)(2,1)S(1)} %get-tuple-element.24), channel_id=1, replica_groups=mesh['row'=8,'col'=4] {'row'}, dimensions={0}, use_global_device_ids=true | all-gather | bytes 147456 | tf_op jit(solution)/shard_map/all_gather | solution.py:10
  50.4 0.2 fusion.15
  50.5 12.0 %all_gather.40 = bf16[64,512]{1,0:T(8,128)(2,1)S(1)} all-gather(bf16[64,128]{1,0:T(8,128)(2,1)S(1)} %get-tuple-element.22), channel_id=1, replica_groups=mesh['row'=8,'col'=4] {'col'}, dimensions={1}, use_global_device_ids=true | all-gather | bytes 81920 | tf_op jit(solution)/shard_map/all_gather | solution.py:32
  62.5 8.2 %all_gather.41 = bf16[512,128]{1,0:T(8,128)(2,1)S(1)} all-gather(bf16[64,128]{1,0:T(8,128)(2,1)S(1)} %get-tuple-element.22), channel_id=1, replica_groups=mesh['row'=8,'col'=4] {'row'}, dimensions={0}, use_global_device_ids=true | all-gather | bytes 147456 | tf_op jit(solution)/shard_map/all_gather | solution.py:10
  70.7 0.2 fusion.14
  70.9 12.0 %all_gather.42 = bf16[64,512]{1,0:T(8,128)(2,1)S(1)} all-gather(bf16[64,128]{1,0:T(8,128)(2,1)S(1)} %get-tuple-element.20), channel_id=1, replica_groups=mesh['row'=8,'col'=4] {'col'}, dimensions={1}, use_global_device_ids=true | all-gather | bytes 81920 | tf_op jit(solution)/shard_map/all_gather | solution.py:32
  82.9 9.2 %all_gather.43 = bf16[512,128]{1,0:T(8,128)(2,1)S(1)} all-gather(bf16[64,128]{1,0:T(8,128)(2,1)S(1)} %get-tuple-element.20), channel_id=1, replica_groups=mesh['row'=8,'col'=4] {'row'}, dimensions={0}, use_global_device_ids=true | all-gather | bytes 147456 | tf_op jit(solution)/shard_map/all_gather | solution.py:10
  92.1 0.2 fusion.13
  92.2 12.0 %all_gather.44 = bf16[64,512]{1,0:T(8,128)(2,1)S(1)} all-gather(bf16[64,128]{1,0:T(8,128)(2,1)S(1)} %get-tuple-element.18), channel_id=1, replica_groups=mesh['row'=8,'col'=4] {'col'}, dimensions={1}, use_global_device_ids=true | all-gather | bytes 81920 | tf_op jit(solution)/shard_map/all_gather | solution.py:32
  104.2 8.2 %all_gather.45 = bf16[512,128]{1,0:T(8,128)(2,1)S(1)} all-gather(bf16[64,128]{1,0:T(8,128)(2,1)S(1)} %get-tuple-element.18), channel_id=1, replica_groups=mesh['row'=8,'col'=4] {'row'}, dimensions={0}, use_global_device_ids=true | all-gather | bytes 147456 | tf_op jit(solution)/shard_map/all_gather | solution.py:10
  112.4 0.2 fusion.12
  112.6 12.0 %all_gather.46 = bf16[64,512]{1,0:T(8,128)(2,1)S(1)} all-gather(bf16[64,128]{1,0:T(8,128)(2,1)S(1)} %get-tuple-element.16), channel_id=1, replica_groups=mesh['row'=8,'col'=4] {'col'}, dimensions={1}, use_global_device_ids=true | all-gather | bytes 81920 | tf_op jit(solution)/shard_map/all_gather | solution.py:32
  124.6 9.2 %all_gather.47 = bf16[512,128]{1,0:T(8,128)(2,1)S(1)} all-gather(bf16[64,128]{1,0:T(8,128)(2,1)S(1)} %get-tuple-element.16), channel_id=1, replica_groups=mesh['row'=8,'col'=4] {'row'}, dimensions={0}, use_global_device_ids=true | all-gather | bytes 147456 | tf_op jit(solution)/shard_map/all_gather | solution.py:10
  133.8 1.5 fusion.10
  135.2 1.3 maximum_bitcast_fusion.5
  136.5 0.1 copy.10
  136.6 1.3 maximum_bitcast_fusion.4
  138.0 0.1 copy.9
  138.1 1.3 maximum_bitcast_fusion.3
  139.4 0.1 copy.8
  139.4 1.3 maximum_bitcast_fusion.2
  140.8 0.1 copy.7
  140.9 1.3 maximum_bitcast_fusion.1
  142.2 0.1 copy.6
  142.3 1.3 maximum_bitcast_fusion
  143.6 0.1 copy.5
  143.7 0.1 stack.99
  143.8 37.7 %psum.7 = f32[6,2]{0,1:T(2,128)S(1)} all-reduce(f32[6,2]{0,1:T(2,128)S(1)} %stack.99), channel_id=1, replica_groups=mesh['row'=8,'col'=4] {'row','col'}, use_global_device_ids=true, to_apply=%region_12.13 | all-reduce | flops 12 | bytes 96 | tf_op jit(solution)/shard_map/psum | solution.py:46
  181.5 0.6 broadcast_multiply_fusion
  (3 shorter events, 0.0 us)
Async XLA Ops:
  0.6 5.5 %copy-start = (f32[64,128]{1,0:T(8,128)S(1)}, f32[64,128]{1,0:T(8,128)}, u32[]{:S(2)}) copy-start(f32[64,128]{1,0:T(8,128)} %param.2) | copy-start | bytes 98308
where the time goes:
time: 183 us; the launch traced here: 182 us
  blocking collectives  165 us (90%)
  other arithmetic  8.46 us (5%)
  between operations  4.56 us (2%)
  matrix products  2.26 us (1%)
  local copies, waits for them, and re-layouts  2.23 us (1%)
    all_gather x6, blocking collectives, body(): row_panel = lax.all_gather(narrow, 'col', axis=1, tiled=True)  73.7 us
    all_gather x6, blocking collectives, taken_in(): lax.all_gather(a, axis, axis=dim, tiled=True)  53.2 us
    psum x1, blocking collectives, body(): stacked = lax.psum(stacked, ('row', 'col'))  37.7 us
    another operation x6, other arithmetic, body(): stacked = jnp.stack(records)  7.88 us

commit v1 on v0

--- a/solution.py
+++ b/solution.py
@@ -43,7 +43,8 @@
         records.append(jnp.stack([plain_local, square_local]))
         density = jnp.where(branch_now == 1, 2.0 * density - square, square)
     stacked = jnp.stack(records)
-    stacked = lax.psum(stacked, ("row", "col"))
+    for over in ("col", "row"):
+        stacked = lax.psum(stacked, over)
     occupations = stacked / size_total
     return (density, occupations)
 

time: 183 us -> 165 us (0.902)
  blocking collectives: 165 us -> 147 us
    psum x1 -> x2, blocking collectives: 37.7 us -> 20.1 us  [body(): stacked = lax.psum(stacked, over)]
where the time goes in v1:
time: 165 us; the launch traced here: 164 us
  blocking collectives  147 us (89%)
  other arithmetic  8.46 us (5%)
  between operations  4.56 us (3%)
  matrix products  2.26 us (1%)
  local copies, waits for them, and re-layouts  2.23 us (1%)
    all_gather x6, blocking collectives, body(): row_panel = lax.all_gather(narrow, 'col', axis=1, tiled=True)  73.7 us
    all_gather x6, blocking collectives, taken_in(): lax.all_gather(a, axis, axis=dim, tiled=True)  53.2 us
    psum x2, blocking collectives, body(): stacked = lax.psum(stacked, over)  20.1 us
    another operation x6, other arithmetic, body(): stacked = jnp.stack(records)  7.88 us

profile of v1, /device:TPU:0, one launch (start us, length us, event | category | flops | bytes accessed | tf_op | source)
XLA Modules:
  0.0 164.5 jit_solution(430901610562500738)
XLA Ops:
  0.6 0.0 copy-start
  0.7 1.6 fusion.17
  6.1 0.0 copy-done
  6.1 13.7 %all_gather.36 = bf16[64,512]{1,0:T(8,128)(2,1)S(1)} all-gather(bf16[64,128]{1,0:T(8,128)(2,1)S(1)} %convert_element_type.19), channel_id=1, replica_groups=mesh['row'=8,'col'=4] {'col'}, dimensions={1}, use_global_device_ids=true | all-gather | bytes 81920 | tf_op jit(solution)/shard_map/all_gather | solution.py:32
  19.8 9.2 %all_gather.37 = bf16[512,128]{1,0:T(8,128)(2,1)S(1)} all-gather(bf16[64,128]{1,0:T(8,128)(2,1)S(1)} %convert_element_type.19), channel_id=1, replica_groups=mesh['row'=8,'col'=4] {'row'}, dimensions={0}, use_global_device_ids=true | all-gather | bytes 147456 | tf_op jit(solution)/shard_map/all_gather | solution.py:10
  29.0 0.2 fusion.16
  29.2 12.0 %all_gather.38 = bf16[64,512]{1,0:T(8,128)(2,1)S(1)} all-gather(bf16[64,128]{1,0:T(8,128)(2,1)S(1)} %get-tuple-element.24), channel_id=1, replica_groups=mesh['row'=8,'col'=4] {'col'}, dimensions={1}, use_global_device_ids=true | all-gather | bytes 81920 | tf_op jit(solution)/shard_map/all_gather | solution.py:32
  41.2 9.2 %all_gather.39 = bf16[512,128]{1,0:T(8,128)(2,1)S(1)} all-gather(bf16[64,128]{1,0:T(8,128)(2,1)S(1)} %get-tuple-element.24), channel_id=1, replica_groups=mesh['row'=8,'col'=4] {'row'}, dimensions={0}, use_global_device_ids=true | all-gather | bytes 147456 | tf_op jit(solution)/shard_map/all_gather | solution.py:10
  50.4 0.2 fusion.15
  50.5 12.0 %all_gather.40 = bf16[64,512]{1,0:T(8,128)(2,1)S(1)} all-gather(bf16[64,128]{1,0:T(8,128)(2,1)S(1)} %get-tuple-element.22), channel_id=1, replica_groups=mesh['row'=8,'col'=4] {'col'}, dimensions={1}, use_global_device_ids=true | all-gather | bytes 81920 | tf_op jit(solution)/shard_map/all_gather | solution.py:32
  62.5 8.2 %all_gather.41 = bf16[512,128]{1,0:T(8,128)(2,1)S(1)} all-gather(bf16[64,128]{1,0:T(8,128)(2,1)S(1)} %get-tuple-element.22), channel_id=1, replica_groups=mesh['row'=8,'col'=4] {'row'}, dimensions={0}, use_global_device_ids=true | all-gather | bytes 147456 | tf_op jit(solution)/shard_map/all_gather | solution.py:10
  70.7 0.2 fusion.14
  70.9 12.0 %all_gather.42 = bf16[64,512]{1,0:T(8,128)(2,1)S(1)} all-gather(bf16[64,128]{1,0:T(8,128)(2,1)S(1)} %get-tuple-element.20), channel_id=1, replica_groups=mesh['row'=8,'col'=4] {'col'}, dimensions={1}, use_global_device_ids=true | all-gather | bytes 81920 | tf_op jit(solution)/shard_map/all_gather | solution.py:32
  82.9 9.2 %all_gather.43 = bf16[512,128]{1,0:T(8,128)(2,1)S(1)} all-gather(bf16[64,128]{1,0:T(8,128)(2,1)S(1)} %get-tuple-element.20), channel_id=1, replica_groups=mesh['row'=8,'col'=4] {'row'}, dimensions={0}, use_global_device_ids=true | all-gather | bytes 147456 | tf_op jit(solution)/shard_map/all_gather | solution.py:10
  92.1 0.2 fusion.13
  92.2 12.0 %all_gather.44 = bf16[64,512]{1,0:T(8,128)(2,1)S(1)} all-gather(bf16[64,128]{1,0:T(8,128)(2,1)S(1)} %get-tuple-element.18), channel_id=1, replica_groups=mesh['row'=8,'col'=4] {'col'}, dimensions={1}, use_global_device_ids=true | all-gather | bytes 81920 | tf_op jit(solution)/shard_map/all_gather | solution.py:32
  104.2 8.2 %all_gather.45 = bf16[512,128]{1,0:T(8,128)(2,1)S(1)} all-gather(bf16[64,128]{1,0:T(8,128)(2,1)S(1)} %get-tuple-element.18), channel_id=1, replica_groups=mesh['row'=8,'col'=4] {'row'}, dimensions={0}, use_global_device_ids=true | all-gather | bytes 147456 | tf_op jit(solution)/shard_map/all_gather | solution.py:10
  112.4 0.2 fusion.12
  112.6 12.0 %all_gather.46 = bf16[64,512]{1,0:T(8,128)(2,1)S(1)} all-gather(bf16[64,128]{1,0:T(8,128)(2,1)S(1)} %get-tuple-element.16), channel_id=1, replica_groups=mesh['row'=8,'col'=4] {'col'}, dimensions={1}, use_global_device_ids=true | all-gather | bytes 81920 | tf_op jit(solution)/shard_map/all_gather | solution.py:32
  124.6 9.2 %all_gather.47 = bf16[512,128]{1,0:T(8,128)(2,1)S(1)} all-gather(bf16[64,128]{1,0:T(8,128)(2,1)S(1)} %get-tuple-element.16), channel_id=1, replica_groups=mesh['row'=8,'col'=4] {'row'}, dimensions={0}, use_global_device_ids=true | all-gather | bytes 147456 | tf_op jit(solution)/shard_map/all_gather | solution.py:10
  133.8 1.5 fusion.10
  135.2 1.3 maximum_bitcast_fusion.5
  136.5 0.1 copy.10
  136.6 1.3 maximum_bitcast_fusion.4
  138.0 0.1 copy.9
  138.1 1.3 maximum_bitcast_fusion.3
  139.4 0.1 copy.8
  139.4 1.3 maximum_bitcast_fusion.2
  140.8 0.1 copy.7
  140.9 1.3 maximum_bitcast_fusion.1
  142.2 0.1 copy.6
  142.3 1.3 maximum_bitcast_fusion
  143.6 0.1 copy.5
  143.7 0.1 stack.99
  143.8 8.3 %psum.14 = f32[6,2]{0,1:T(2,128)S(1)} all-reduce(f32[6,2]{0,1:T(2,128)S(1)} %stack.99), channel_id=1, replica_groups=mesh['row'=8,'col'=4] {'col'}, use_global_device_ids=true, to_apply=%region_12.13 | all-reduce | flops 12 | bytes 96 | tf_op jit(solution)/shard_map/psum | solution.py:47
  152.1 11.8 %psum.15 = f32[6,2]{0,1:T(2,128)S(1)} all-reduce(f32[6,2]{0,1:T(2,128)S(1)} %psum.14), channel_id=1, replica_groups=mesh['row'=8,'col'=4] {'row'}, use_global_device_ids=true, to_apply=%region_13.14 | all-reduce | flops 12 | bytes 96 | tf_op jit(solution)/shard_map/psum | solution.py:47
  163.9 0.6 broadcast_multiply_fusion
  (3 shorter events, 0.0 us)
Async XLA Ops:
  0.6 5.5 %copy-start = (f32[64,128]{1,0:T(8,128)S(1)}, f32[64,128]{1,0:T(8,128)}, u32[]{:S(2)}) copy-start(f32[64,128]{1,0:T(8,128)} %param.2) | copy-start | bytes 98308
